TPU v7x, 32 devices: a whole 2x2x4 slice. The times are simulated.
32 devices in a mesh: items: 8 (over z, y), users: 4 (over x, core).
Axes of the slice: x: 2, y: 2, z: 4, core: 2. Of those that a mesh axis runs over, the one named last changes fastest.
Arguments:
- user_emb: bfloat16 [4096, 256], P('users', 'items'), as said below
- item_emb: bfloat16 [262144, 256], P('items'), as said below
- target: int32 [4096], P('users'), may hold values from 0 to 262143
- history: int32 [4096, 32], P('users'), may hold values from 0 to 262143, as said below
Outputs:
- log_rank: float32 [4096], P('users')
- metrics: float32 [2], replicated
Inputs may be any that keep to these rules, and one draw needn't show every extreme that they name: history[u, k] lies in [k * 8192, (k + 1) * 8192); a user's history entries are thus distinct. `item_emb`: rows of norm about one. `user_emb`: entries of order one.
All inputs are finite; a program needn't handle non-finite values.
Results may differ from a plain program's by a relative error of at most 0.0003.
Values may be sent and summed in bfloat16 or wider, within the bound.
A program may use at most 64 MiB of HBM per device.

v0:
```python
import jax
import jax.numpy as jnp
from jax import lax
from jax.sharding import PartitionSpec as P

sharpness = 4.0


def body(user_emb, item_emb, target, history):
    item_dev = item_emb.shape[0]
    shard = lax.axis_index("items")
    start = shard * item_dev
    local_t = target - start
    inside = (local_t >= 0) & (local_t < item_dev)
    own_rows = item_emb[jnp.clip(local_t, 0, item_dev - 1)]
    users = lax.all_gather(user_emb, "items", axis=1, tiled=True)
    partial_t = jnp.sum(users.astype(jnp.float32) * own_rows.astype(jnp.float32), axis=1)
    tscore = lax.psum(jnp.where(inside, partial_t, 0.0), "items")
    n_items = lax.axis_size("items")
    n_users = lax.axis_size("users")
    u_dev = users.shape[0]
    blk = min(item_dev, 4096)
    nblk = item_dev // blk

    def add_block(index, total):
        rows = lax.dynamic_slice_in_dim(item_emb, index * blk, blk, 0)
        score = lax.dot_general(
            users, rows, (((1,), (1,)), ((), ())), preferred_element_type=jnp.float32
        )
        return total + jnp.sum(jax.nn.sigmoid(sharpness * (score - tscore[:, None])), axis=1)

    total = lax.fori_loop(0, nblk, add_block, jnp.zeros((u_dev,), jnp.float32))
    per_shard = history.shape[1] // n_items
    own_hist = lax.dynamic_slice_in_dim(history, shard * per_shard, per_shard, 1)
    hrows = item_emb[own_hist - start]
    hscore = jnp.einsum("ud,uhd->uh", users, hrows, preferred_element_type=jnp.float32)
    local = total - jnp.sum(jax.nn.sigmoid(sharpness * (hscore - tscore[:, None])), axis=1)
    seen = jnp.any(history == target[:, None], axis=1)
    correction = jnp.where(seen, 0.0, 0.5).astype(jnp.float32)
    all_users = u_dev * n_users
    above = lax.psum(local, "items") - correction
    rank = 1.0 + above
    log_rank = jnp.log(rank)
    hit = jax.nn.sigmoid(10.5 - rank)
    gain = hit / jnp.log2(1.0 + rank)
    hit_sum, gain_sum = lax.psum((jnp.sum(hit), jnp.sum(gain)), "users")
    metrics = jnp.stack([hit_sum, gain_sum]) / all_users
    return (log_rank, metrics)


def solution(mesh):
    return jax.shard_map(
        body,
        mesh=mesh,
        in_specs=(P("users", "items"), P("items", None), P("users"), P("users", None)),
        out_specs=(P("users"), P()),
        check_vma=False,
    )
```

profile of v0, /device:TPU:0, one launch (start us, length us, event | category | flops | bytes accessed | tf_op | source)
XLA Modules:
  0.0 174.1 jit_solution(5118468006411309888)
XLA Ops:
  0.6 0.0 copy-start.1
  0.6 0.0 copy-start.2
  0.7 0.8 compare_select_fusion
  1.5 0.2 copy.14
  1.7 0.3 reshape.17
  2.0 20.9 %gather_fusion.1 = bf16[4096,256]{1,0:T(8,128)(2,1)S(1)} fusion(bf16[32768,256]{1,0:T(8,128)(2,1)} %param.7, s32[4096]{0:T(1024)S(1)} %broadcast_clamp_fusion), kind=kCustom, calls=%fused_computation.1 | custom fusion | bytes 4210688 | tf_op jit(solution)/shard_map/gather | solution.py:35
  22.9 2.1 %reshape.16 = bf16[1024,4,256]{2,1,0:T(4,128)(2,1)} reshape(bf16[4096,256]{1,0:T(8,128)(2,1)S(1)} %gather_fusion.1) | data formatting | bytes 4194304 | tf_op jit(solution)/shard_map/gather | solution.py:35
  25.0 0.0 copy-done.1
  25.0 33.0 %all_gather.3 = bf16[1024,256]{0,1:T(8,128)(2,1)S(1)} all-gather(bf16[1024,32]{0,1:T(8,128)(2,1)S(1)} %copy-done.1), channel_id=1, replica_groups=mesh['items'=8,'users'=4] {'items'}, dimensions={1}, use_global_device_ids=true | all-gather | bytes 589824 | tf_op jit(solution)/shard_map/all_gather | solution.py:16
  58.0 0.2 copy.20
  58.2 2.9 %multiply_reduce_fusion = f32[1024,4]{1,0:T(8,128)S(1)} fusion(f32[1024,256]{1,0:T(8,128)S(1)} %copy.20, bf16[1024,4,256]{2,1,0:T(4,128)(2,1)} %reshape.16), kind=kLoop, calls=%fused_computation.7 | loop fusion | flops 3141632 | bytes 3162112
  61.1 0.2 copy.19
  61.3 0.0 copy-done.2
  61.3 11.4 %gather_fusion = bf16[1024,256]{1,0:T(8,128)(2,1)S(1)} fusion(bf16[32768,256]{1,0:T(8,128)(2,1)} %param.7, s32[1024]{0:T(1024)S(1)} %fusion.4), kind=kCustom, calls=%fused_computation | custom fusion | bytes 1052672 | tf_op jit(solution)/shard_map/gather | solution.py:15
  72.7 0.2 copy.13
  73.0 0.2 multiply_reduce_fusion.1
  73.2 21.5 %psum.28 = f32[1024]{0:T(1024)S(1)} all-reduce(f32[1024]{0:T(1024)S(1)} %and_select_fusion), channel_id=1, replica_groups=mesh['items'=8,'users'=4] {'items'}, use_global_device_ids=true, to_apply=%region_1.2 | all-reduce | flops 1024 | bytes 8192 | tf_op jit(solution)/shard_map/psum | solution.py:18
  94.8 0.0 copy-start
  94.8 52.7 %while.14 = (s32[]{:T(128)}, f32[1024]{0:T(1024)S(1)}, bf16[32768,256]{1,0:T(8,128)(2,1)}, bf16[1024,256]{1,0:T(8,128)(2,1)S(1)}, f32[1024]{0:T(1024)S(1)}, /*index=5*/s32[]{:T(128)}, s32[]{:T(128)}, s32[]{:T(128)}, s32[]{:T(128)}) while((s32[]{:T(128)}, f32[1024]{0:T(1024)S(1)}, bf16[32768,256]{1,0:T(8,128)(2,1)}, ...), condition=%wide.region_4.5_spmd.clone, body=%wide.region_2.4_spmd.clone.sunk | while | flops 2172650496 | bytes 2642073 | solution.py:32
  94.8 6.6 %fusion.11 = f32[1024]{0:T(1024)S(1)} fusion(bf16[1024,256]{1,0:T(8,128)(2,1)S(1)} %get-tuple-element.192, f32[1024]{0:T(1024)S(1)} %get-tuple-element.193, bf16[32768,256]{1,0:T(8,128)(2,1)} %get-tuple-element.191, s32[]{:T(128)S(6)} %select_n.43), kind=kOutput, calls=%fused_computation.3.clone.1 | convolution fusion | flops 2172648448 | bytes 2629636 | tf_op jit(solution)/shard_map/while/body/eval_jaxpr/dot_general | solution.py:27
  101.4 6.5 %fusion.11 = f32[1024]{0:T(1024)S(1)} fusion(bf16[1024,256]{1,0:T(8,128)(2,1)S(1)} %get-tuple-element.192, f32[1024]{0:T(1024)S(1)} %get-tuple-element.193, bf16[32768,256]{1,0:T(8,128)(2,1)} %get-tuple-element.191, s32[]{:T(128)S(6)} %select_n.43), kind=kOutput, calls=%fused_computation.3.clone.1 | convolution fusion | flops 2172648448 | bytes 2629636 | tf_op jit(solution)/shard_map/while/body/eval_jaxpr/dot_general | solution.py:27
  108.0 6.5 %fusion.11 = f32[1024]{0:T(1024)S(1)} fusion(bf16[1024,256]{1,0:T(8,128)(2,1)S(1)} %get-tuple-element.192, f32[1024]{0:T(1024)S(1)} %get-tuple-element.193, bf16[32768,256]{1,0:T(8,128)(2,1)} %get-tuple-element.191, s32[]{:T(128)S(6)} %select_n.43), kind=kOutput, calls=%fused_computation.3.clone.1 | convolution fusion | flops 2172648448 | bytes 2629636 | tf_op jit(solution)/shard_map/while/body/eval_jaxpr/dot_general | solution.py:27
  114.6 6.5 %fusion.11 = f32[1024]{0:T(1024)S(1)} fusion(bf16[1024,256]{1,0:T(8,128)(2,1)S(1)} %get-tuple-element.192, f32[1024]{0:T(1024)S(1)} %get-tuple-element.193, bf16[32768,256]{1,0:T(8,128)(2,1)} %get-tuple-element.191, s32[]{:T(128)S(6)} %select_n.43), kind=kOutput, calls=%fused_computation.3.clone.1 | convolution fusion | flops 2172648448 | bytes 2629636 | tf_op jit(solution)/shard_map/while/body/eval_jaxpr/dot_general | solution.py:27
  121.2 6.5 %fusion.11 = f32[1024]{0:T(1024)S(1)} fusion(bf16[1024,256]{1,0:T(8,128)(2,1)S(1)} %get-tuple-element.192, f32[1024]{0:T(1024)S(1)} %get-tuple-element.193, bf16[32768,256]{1,0:T(8,128)(2,1)} %get-tuple-element.191, s32[]{:T(128)S(6)} %select_n.43), kind=kOutput, calls=%fused_computation.3.clone.1 | convolution fusion | flops 2172648448 | bytes 2629636 | tf_op jit(solution)/shard_map/while/body/eval_jaxpr/dot_general | solution.py:27
  127.8 6.5 %fusion.11 = f32[1024]{0:T(1024)S(1)} fusion(bf16[1024,256]{1,0:T(8,128)(2,1)S(1)} %get-tuple-element.192, f32[1024]{0:T(1024)S(1)} %get-tuple-element.193, bf16[32768,256]{1,0:T(8,128)(2,1)} %get-tuple-element.191, s32[]{:T(128)S(6)} %select_n.43), kind=kOutput, calls=%fused_computation.3.clone.1 | convolution fusion | flops 2172648448 | bytes 2629636 | tf_op jit(solution)/shard_map/while/body/eval_jaxpr/dot_general | solution.py:27
  134.4 6.5 %fusion.11 = f32[1024]{0:T(1024)S(1)} fusion(bf16[1024,256]{1,0:T(8,128)(2,1)S(1)} %get-tuple-element.192, f32[1024]{0:T(1024)S(1)} %get-tuple-element.193, bf16[32768,256]{1,0:T(8,128)(2,1)} %get-tuple-element.191, s32[]{:T(128)S(6)} %select_n.43), kind=kOutput, calls=%fused_computation.3.clone.1 | convolution fusion | flops 2172648448 | bytes 2629636 | tf_op jit(solution)/shard_map/while/body/eval_jaxpr/dot_general | solution.py:27
  140.9 6.5 %fusion.11 = f32[1024]{0:T(1024)S(1)} fusion(bf16[1024,256]{1,0:T(8,128)(2,1)S(1)} %get-tuple-element.192, f32[1024]{0:T(1024)S(1)} %get-tuple-element.193, bf16[32768,256]{1,0:T(8,128)(2,1)} %get-tuple-element.191, s32[]{:T(128)S(6)} %select_n.43), kind=kOutput, calls=%fused_computation.3.clone.1 | convolution fusion | flops 2172648448 | bytes 2629636 | tf_op jit(solution)/shard_map/while/body/eval_jaxpr/dot_general | solution.py:27
  147.5 17.1 %psum.29 = f32[1024]{0:T(1024)S(1)} all-reduce(f32[1024]{0:T(1024)S(1)} %sub.59), channel_id=1, replica_groups=mesh['items'=8,'users'=4] {'items'}, use_global_device_ids=true, to_apply=%region_6.7 | all-reduce | flops 1024 | bytes 8192 | tf_op jit(solution)/shard_map/psum | solution.py:41
  164.7 0.0 copy-done
  164.7 1.3 divide_reduce_fusion.1
  166.0 6.3 %all-reduce = (f32[1]{0:T(128)}, f32[1]{0:T(128)}) all-reduce(f32[1]{0:T(128)} %bitcast.2, f32[1]{0:T(128)} %bitcast.1), channel_id=1, replica_groups=mesh['items'=8,'users'=4] {'users'}, use_global_device_ids=true, to_apply=%region_11.12 | all-reduce | flops 2 | bytes 16 | tf_op jit(solution)/shard_map/psum | solution.py:46
  172.3 1.8 %maximum_multiply_fusion = f32[2]{0:T(128)} fusion(f32[1]{0:T(128)} %get-tuple-element.137, f32[1]{0:T(128)} %get-tuple-element.138), kind=kLoop, calls=%fused_computation.22 | loop fusion | flops 4 | bytes 16 | tf_op jit(solution)/shard_map/div | solution.py:47
  (15 shorter events, 0.1 us)
Async XLA Ops:
  0.6 24.4 %copy-start.1 = (bf16[1024,32]{0,1:T(8,128)(2,1)S(1)}, bf16[1024,32]{0,1:T(8,128)(2,1)}, u32[]{:S(2)}) copy-start(bf16[1024,32]{0,1:T(8,128)(2,1)} %param.6) | copy-start | bytes 196612
  0.6 60.7 %copy-start.2 = (s32[1024]{0:T(1024)S(1)}, s32[1024]{0:T(1024)}, u32[]{:S(2)}) copy-start(s32[1024]{0:T(1024)} %param.8) | copy-start | bytes 12292
  94.8 69.9 %copy-start = (s32[1024,32]{0,1:T(8,128)S(1)}, s32[1024,32]{0,1:T(8,128)}, u32[]{:S(2)}) copy-start(s32[1024,32]{0,1:T(8,128)} %param.9) | copy-start | bytes 393220
where the time goes:
time: 175 us; the launch traced here: 174 us
  blocking collectives  78 us (45%)
  matrix products  52.4 us (30%)
  local copies, waits for them, and re-layouts  35.5 us (20%)
  other arithmetic  7.14 us (4%)
    dot_general x8, matrix products, add_block(): lax.dot_general(users, rows, (((1,), (1,)), ((), ())), preferred_element_...  52.4 us
    all_gather x1, blocking collectives, body(): users = lax.all_gather(user_emb, 'items', axis=1, tiled=True)  33 us
    gather x2, local copies, waits for them, and re-layouts, body(): hrows = item_emb[own_hist - start]  23 us
    psum x1, blocking collectives, body(): tscore = lax.psum(jnp.where(inside, partial_t, 0.0), 'items')  21.5 us
    psum x1, blocking collectives, body(): above = lax.psum(local, 'items') - correction  17.1 us
    gather x1, local copies, waits for them, and re-layouts, body(): own_rows = item_emb[jnp.clip(local_t, 0, item_dev - 1)]  11.4 us
    psum x1, blocking collectives, body(): hit_sum, gain_sum = lax.psum((jnp.sum(hit), jnp.sum(gain)), 'users')  6.3 us

commit v1 on v0

--- a/solution.py
+++ b/solution.py
@@ -15,7 +15,9 @@
     own_rows = item_emb[jnp.clip(local_t, 0, item_dev - 1)]
     users = lax.all_gather(user_emb, "items", axis=1, tiled=True)
     partial_t = jnp.sum(users.astype(jnp.float32) * own_rows.astype(jnp.float32), axis=1)
-    tscore = lax.psum(jnp.where(inside, partial_t, 0.0), "items")
+    part = jnp.where(inside, partial_t, 0.0)
+    blocks = lax.all_gather(part, "items", axis=0, tiled=False)
+    tscore = blocks.sum(axis=0)
     n_items = lax.axis_size("items")
     n_users = lax.axis_size("users")
     u_dev = users.shape[0]

time: 175 us -> 188 us (1.074)
  blocking collectives: 78 us -> 91.5 us
    all_gather x0 -> x1, blocking collectives: none -> 30.6 us  [body(): blocks = lax.all_gather(part, 'items', axis=0, tiled=False)]
    psum x1 -> x0, blocking collectives: 21.5 us -> none  [body(): tscore = lax.psum(jnp.where(inside, partial_t, 0.0), 'items')]
    psum x1, blocking collectives: 17.1 us -> 21.5 us  [body(): above = lax.psum(local, 'items') - correction]
where the time goes in v1:
time: 188 us
  blocking collectives  91.5 us (49%)
  matrix products  52.3 us (28%)
  local copies, waits for them, and re-layouts  35.5 us (19%)
  other arithmetic  7.15 us (4%)
    dot_general x8, matrix products, add_block(): lax.dot_general(users, rows, (((1,), (1,)), ((), ())), preferred_element_...  52.3 us
    all_gather x1, blocking collectives, body(): users = lax.all_gather(user_emb, 'items', axis=1, tiled=True)  33 us
    all_gather x1, blocking collectives, body(): blocks = lax.all_gather(part, 'items', axis=0, tiled=False)  30.6 us
    gather x2, local copies, waits for them, and re-layouts, body(): hrows = item_emb[own_hist - start]  23 us
    psum x1, blocking collectives, body(): above = lax.psum(local, 'items') - correction  21.5 us
    gather x1, local copies, waits for them, and re-layouts, body(): own_rows = item_emb[jnp.clip(local_t, 0, item_dev - 1)]  11.4 us
    psum x1, blocking collectives, body(): hit_sum, gain_sum = lax.psum((jnp.sum(hit), jnp.sum(gain)), 'users')  6.3 us

profile of v1, /device:TPU:0, one launch (start us, length us, event | category | flops | bytes accessed | tf_op | source)
XLA Modules:
  0.0 187.6 jit_solution(13013447190259843007)
XLA Ops:
  0.6 0.0 copy-start.1
  0.6 0.0 copy-start.2
  0.7 0.8 compare_select_fusion
  1.5 0.2 copy.14
  1.7 0.3 reshape.17
  2.0 20.9 %gather_fusion.1 = bf16[4096,256]{1,0:T(8,128)(2,1)S(1)} fusion(bf16[32768,256]{1,0:T(8,128)(2,1)} %param.7, s32[4096]{0:T(1024)S(1)} %broadcast_clamp_fusion), kind=kCustom, calls=%fused_computation.1 | custom fusion | bytes 4210688 | tf_op jit(solution)/shard_map/gather | solution.py:37
  22.9 2.1 %reshape.16 = bf16[1024,4,256]{2,1,0:T(4,128)(2,1)} reshape(bf16[4096,256]{1,0:T(8,128)(2,1)S(1)} %gather_fusion.1) | data formatting | bytes 4194304 | tf_op jit(solution)/shard_map/gather | solution.py:37
  25.0 0.0 copy-done.1
  25.0 33.0 %all_gather.9 = bf16[1024,256]{0,1:T(8,128)(2,1)S(1)} all-gather(bf16[1024,32]{0,1:T(8,128)(2,1)S(1)} %copy-done.1), channel_id=1, replica_groups=mesh['items'=8,'users'=4] {'items'}, dimensions={1}, use_global_device_ids=true | all-gather | bytes 589824 | tf_op jit(solution)/shard_map/all_gather | solution.py:16
  58.0 0.2 copy.20
  58.2 2.9 %multiply_reduce_fusion = f32[1024,4]{1,0:T(8,128)S(1)} fusion(f32[1024,256]{1,0:T(8,128)S(1)} %copy.20, bf16[1024,4,256]{2,1,0:T(4,128)(2,1)} %reshape.16), kind=kLoop, calls=%fused_computation.7 | loop fusion | flops 3141632 | bytes 3162112
  61.1 0.2 copy.19
  61.3 0.0 copy-done.2
  61.3 11.4 %gather_fusion = bf16[1024,256]{1,0:T(8,128)(2,1)S(1)} fusion(bf16[32768,256]{1,0:T(8,128)(2,1)} %param.7, s32[1024]{0:T(1024)S(1)} %fusion.4), kind=kCustom, calls=%fused_computation | custom fusion | bytes 1052672 | tf_op jit(solution)/shard_map/gather | solution.py:15
  72.7 0.2 copy.13
  73.0 0.2 multiply_reduce_fusion.1
  73.2 30.6 %all-gather = f32[8192]{0:T(1024)S(1)} all-gather(f32[1024]{0:T(1024)S(1)} %and_select_fusion), channel_id=2, replica_groups=mesh['items'=8,'users'=4] {'items'}, dimensions={0}, use_global_device_ids=true | all-gather | bytes 36864 | tf_op jit(solution)/shard_map/all_gather | solution.py:19
  103.9 0.0 copy-start
  103.9 52.7 %while.14 = (s32[]{:T(128)}, f32[1024]{0:T(1024)S(1)}, bf16[32768,256]{1,0:T(8,128)(2,1)}, bf16[1024,256]{1,0:T(8,128)(2,1)S(1)}, f32[1024]{0:T(1024)S(1)}, /*index=5*/s32[]{:T(128)}, s32[]{:T(128)}, s32[]{:T(128)}, s32[]{:T(128)}) while((s32[]{:T(128)}, f32[1024]{0:T(1024)S(1)}, bf16[32768,256]{1,0:T(8,128)(2,1)}, ...), condition=%wide.region_4.5_spmd.clone, body=%wide.region_2.4_spmd.clone.sunk | while | flops 2172650496 | bytes 2642073 | solution.py:34
  103.9 6.6 %fusion.11 = f32[1024]{0:T(1024)S(1)} fusion(bf16[1024,256]{1,0:T(8,128)(2,1)S(1)} %get-tuple-element.192, f32[1024]{0:T(1024)S(1)} %get-tuple-element.193, bf16[32768,256]{1,0:T(8,128)(2,1)} %get-tuple-element.191, s32[]{:T(128)S(6)} %select_n.43), kind=kOutput, calls=%fused_computation.3.clone.1 | convolution fusion | flops 2172648448 | bytes 2629636 | tf_op jit(solution)/shard_map/while/body/eval_jaxpr/dot_general | solution.py:29
  110.5 6.5 %fusion.11 = f32[1024]{0:T(1024)S(1)} fusion(bf16[1024,256]{1,0:T(8,128)(2,1)S(1)} %get-tuple-element.192, f32[1024]{0:T(1024)S(1)} %get-tuple-element.193, bf16[32768,256]{1,0:T(8,128)(2,1)} %get-tuple-element.191, s32[]{:T(128)S(6)} %select_n.43), kind=kOutput, calls=%fused_computation.3.clone.1 | convolution fusion | flops 2172648448 | bytes 2629636 | tf_op jit(solution)/shard_map/while/body/eval_jaxpr/dot_general | solution.py:29
  117.1 6.5 %fusion.11 = f32[1024]{0:T(1024)S(1)} fusion(bf16[1024,256]{1,0:T(8,128)(2,1)S(1)} %get-tuple-element.192, f32[1024]{0:T(1024)S(1)} %get-tuple-element.193, bf16[32768,256]{1,0:T(8,128)(2,1)} %get-tuple-element.191, s32[]{:T(128)S(6)} %select_n.43), kind=kOutput, calls=%fused_computation.3.clone.1 | convolution fusion | flops 2172648448 | bytes 2629636 | tf_op jit(solution)/shard_map/while/body/eval_jaxpr/dot_general | solution.py:29
  123.7 6.5 %fusion.11 = f32[1024]{0:T(1024)S(1)} fusion(bf16[1024,256]{1,0:T(8,128)(2,1)S(1)} %get-tuple-element.192, f32[1024]{0:T(1024)S(1)} %get-tuple-element.193, bf16[32768,256]{1,0:T(8,128)(2,1)} %get-tuple-element.191, s32[]{:T(128)S(6)} %select_n.43), kind=kOutput, calls=%fused_computation.3.clone.1 | convolution fusion | flops 2172648448 | bytes 2629636 | tf_op jit(solution)/shard_map/while/body/eval_jaxpr/dot_general | solution.py:29
  130.3 6.5 %fusion.11 = f32[1024]{0:T(1024)S(1)} fusion(bf16[1024,256]{1,0:T(8,128)(2,1)S(1)} %get-tuple-element.192, f32[1024]{0:T(1024)S(1)} %get-tuple-element.193, bf16[32768,256]{1,0:T(8,128)(2,1)} %get-tuple-element.191, s32[]{:T(128)S(6)} %select_n.43), kind=kOutput, calls=%fused_computation.3.clone.1 | convolution fusion | flops 2172648448 | bytes 2629636 | tf_op jit(solution)/shard_map/while/body/eval_jaxpr/dot_general | solution.py:29
  136.9 6.5 %fusion.11 = f32[1024]{0:T(1024)S(1)} fusion(bf16[1024,256]{1,0:T(8,128)(2,1)S(1)} %get-tuple-element.192, f32[1024]{0:T(1024)S(1)} %get-tuple-element.193, bf16[32768,256]{1,0:T(8,128)(2,1)} %get-tuple-element.191, s32[]{:T(128)S(6)} %select_n.43), kind=kOutput, calls=%fused_computation.3.clone.1 | convolution fusion | flops 2172648448 | bytes 2629636 | tf_op jit(solution)/shard_map/while/body/eval_jaxpr/dot_general | solution.py:29
  143.5 6.5 %fusion.11 = f32[1024]{0:T(1024)S(1)} fusion(bf16[1024,256]{1,0:T(8,128)(2,1)S(1)} %get-tuple-element.192, f32[1024]{0:T(1024)S(1)} %get-tuple-element.193, bf16[32768,256]{1,0:T(8,128)(2,1)} %get-tuple-element.191, s32[]{:T(128)S(6)} %select_n.43), kind=kOutput, calls=%fused_computation.3.clone.1 | convolution fusion | flops 2172648448 | bytes 2629636 | tf_op jit(solution)/shard_map/while/body/eval_jaxpr/dot_general | solution.py:29
  150.0 6.5 %fusion.11 = f32[1024]{0:T(1024)S(1)} fusion(bf16[1024,256]{1,0:T(8,128)(2,1)S(1)} %get-tuple-element.192, f32[1024]{0:T(1024)S(1)} %get-tuple-element.193, bf16[32768,256]{1,0:T(8,128)(2,1)} %get-tuple-element.191, s32[]{:T(128)S(6)} %select_n.43), kind=kOutput, calls=%fused_computation.3.clone.1 | convolution fusion | flops 2172648448 | bytes 2629636 | tf_op jit(solution)/shard_map/while/body/eval_jaxpr/dot_general | solution.py:29
  156.6 21.5 %psum.21 = f32[1024]{0:T(1024)S(1)} all-reduce(f32[1024]{0:T(1024)S(1)} %sub.59), channel_id=1, replica_groups=mesh['items'=8,'users'=4] {'items'}, use_global_device_ids=true, to_apply=%region_6.7 | all-reduce | flops 1024 | bytes 8192 | tf_op jit(solution)/shard_map/psum | solution.py:43
  178.2 0.0 copy-done
  178.2 1.3 divide_reduce_fusion.1
  179.5 6.3 %all-reduce = (f32[1]{0:T(128)}, f32[1]{0:T(128)}) all-reduce(f32[1]{0:T(128)} %bitcast.2, f32[1]{0:T(128)} %bitcast.1), channel_id=1, replica_groups=mesh['items'=8,'users'=4] {'users'}, use_global_device_ids=true, to_apply=%region_11.12 | all-reduce | flops 2 | bytes 16 | tf_op jit(solution)/shard_map/psum | solution.py:48
  185.8 1.8 maximum_multiply_fusion
  (17 shorter events, 0.2 us)
Async XLA Ops:
  0.6 24.4 %copy-start.1 = (bf16[1024,32]{0,1:T(8,128)(2,1)S(1)}, bf16[1024,32]{0,1:T(8,128)(2,1)}, u32[]{:S(2)}) copy-start(bf16[1024,32]{0,1:T(8,128)(2,1)} %param.6) | copy-start | bytes 196612
  0.6 60.7 %copy-start.2 = (s32[1024]{0:T(1024)S(1)}, s32[1024]{0:T(1024)}, u32[]{:S(2)}) copy-start(s32[1024]{0:T(1024)} %param.8) | copy-start | bytes 12292
  103.9 74.3 %copy-start = (s32[1024,32]{0,1:T(8,128)S(1)}, s32[1024,32]{0,1:T(8,128)}, u32[]{:S(2)}) copy-start(s32[1024,32]{0,1:T(8,128)} %param.9) | copy-start | bytes 393220
